TPU v7x, 32 devices: a whole 2x2x4 slice. The times are simulated.
32 devices in a mesh: rep: 2 (over core), ep: 16 (over z, y, x).
Axes of the slice: x: 2, y: 2, z: 4, core: 2. Of those that a mesh axis runs over, the one named last changes fastest.
Arguments:
- tokens: bfloat16 [4096, 2048], P(('rep', 'ep')), may hold values from -6 to 6
- gates: float32 [4096], P(('rep', 'ep')), may hold values from 0.25 to 1
- expert_ids: int32 [4096, 1], P(('rep', 'ep')), may hold values from 0 to 3; in each aligned block of 128 rows (0 to 127, 128 to 255, ...) at most 40 rows name the same one
- weight_in: bfloat16 [2048, 16384], P(None, 'ep'), may hold values from -0.125 to 0.125
- weight_out: bfloat16 [16384, 2048], P('ep'), may hold values from -0.09375 to 0.09375
Outputs:
- mixed: bfloat16 [4096, 2048], P(('rep', 'ep'))
Inputs may be any that keep to these rules, and one draw needn't show every extreme that they name: `expert_ids`: among the 128 rows of one device no expert is named by more than 40 rows, and some expert is named by exactly that many in some devices' rows; every expert is named somewhere.
All inputs are finite; a program needn't handle non-finite values.
Results may differ from a plain program's by a relative error of at most 0.0057.
Values may be sent and summed in bfloat16 or wider, within the bound.
No kernel may reach another device: no remote copies, remote signals or barrier semaphores. Data moves between devices by JAX's collectives and lax.ppermute only.
A program may use at most 64 MiB of HBM per device.

v0:
```python
import jax
import jax.numpy as jnp
from jax import lax
from jax.sharding import PartitionSpec as P

SLICES = 4


def from_partner(block, axis, distance):
    count = lax.axis_size(axis)
    route = []
    for low in range(count):
        high = low | 1 << distance
        if high != low and high < count:
            route += [(low, high), (high, low)]
    return lax.ppermute(block, axis, route)


def feed(rows, weight_in, weight_out):
    shape = rows.shape
    flat = rows.reshape(-1, shape[-1])
    hidden = jnp.maximum(jnp.dot(flat, weight_in, preferred_element_type=jnp.float32), 0.0).astype(
        jnp.bfloat16
    )
    result = jnp.dot(hidden, weight_out, preferred_element_type=jnp.float32).astype(jnp.bfloat16)
    return result.reshape(shape[:-1] + (weight_out.shape[1],))


def body(tokens, gates, expert_ids, weight_in, weight_out):
    owner_count = lax.axis_size("ep")
    experts = owner_count // SLICES
    tok_rows = tokens.shape[0]
    width = tokens.shape[1]
    capacity = 3 * tok_rows // (4 * experts)
    spare = tok_rows // (2 * experts)
    expert_of = expert_ids[:, 0]
    same = expert_of[:, None] == expert_of[None, :]
    before = lax.broadcasted_iota(jnp.int32, (tok_rows, tok_rows), 1) < lax.broadcasted_iota(
        jnp.int32, (tok_rows, tok_rows), 0
    )
    place_rank = jnp.sum((same & before).astype(jnp.int32), axis=1)
    spilled = place_rank >= capacity
    seat_pos = jnp.where(spilled, place_rank - capacity, place_rank)
    main_slot = jnp.where(spilled, experts * capacity, expert_of * capacity + seat_pos)
    extra_slot = jnp.where(spilled, expert_of * spare + seat_pos, experts * spare)
    main_buffer = (
        jnp.zeros((experts * capacity + 1, width), jnp.bfloat16).at[main_slot].set(tokens)[:-1]
    )
    extra_buffer = (
        jnp.zeros((experts * spare + 1, width), jnp.bfloat16).at[extra_slot].set(tokens)[:-1]
    )
    quarter = width // SLICES
    lane = lax.axis_index("ep") % SLICES
    low_bit = lane % 2
    high_bit = lane // 2

    def narrow(buffer, seats):
        return (
            buffer.reshape(experts, seats, SLICES, quarter)
            .transpose(0, 2, 1, 3)
            .reshape(owner_count, seats, quarter)
        )

    def widen(rows, seats):
        return (
            rows.reshape(experts, SLICES, seats, quarter)
            .transpose(0, 2, 1, 3)
            .reshape(experts * seats, width)
        )

    def gather_group(rows):
        other = from_partner(rows, "ep", 0)
        pair = jnp.where(low_bit == 0, jnp.stack([rows, other], -2), jnp.stack([other, rows], -2))
        across = from_partner(pair, "ep", 1)
        whole = jnp.where(
            high_bit == 0, jnp.stack([pair, across], -3), jnp.stack([across, pair], -3)
        )
        return whole.reshape(rows.shape[:-1] + (width,))

    def reduce_group(part):
        split = part.reshape(part.shape[:-1] + (2, 2, quarter))
        keep = lax.dynamic_index_in_dim(split, high_bit, 2, keepdims=False)
        sending = lax.dynamic_index_in_dim(split, 1 - high_bit, 2, keepdims=False)
        landed = from_partner(sending, "ep", 1)
        both = jnp.stack([keep, landed], 0)
        mine = lax.dynamic_index_in_dim(both, low_bit, 3, keepdims=False)
        giving = lax.dynamic_index_in_dim(both, 1 - low_bit, 3, keepdims=False)
        taken = from_partner(giving, "ep", 0)
        return jnp.sum(mine.astype(jnp.float32), axis=0) + jnp.sum(
            taken.astype(jnp.float32), axis=0
        )

    summed = reduce_group(
        feed(
            gather_group(
                lax.all_to_all(
                    narrow(main_buffer, capacity), "ep", split_axis=0, concat_axis=0, tiled=True
                )
            ),
            weight_in,
            weight_out,
        )
    )
    own_rows = lax.all_to_all(summed, "ep", split_axis=0, concat_axis=0, tiled=True)
    moved_rows = from_partner(narrow(extra_buffer, spare), "rep", 0)
    summed = reduce_group(
        feed(
            gather_group(lax.all_to_all(moved_rows, "ep", split_axis=0, concat_axis=0, tiled=True)),
            weight_in,
            weight_out,
        )
    )
    far_rows = lax.all_to_all(
        summed.astype(jnp.bfloat16), "ep", split_axis=0, concat_axis=0, tiled=True
    ).astype(summed.dtype)
    far_sums = from_partner(far_rows.astype(jnp.bfloat16), "rep", 0).astype(far_rows.dtype)
    combined = jnp.concatenate([widen(own_rows, capacity), widen(far_sums, spare)], axis=0)
    row_index = jnp.where(
        spilled, experts * capacity + expert_of * spare + seat_pos, expert_of * capacity + seat_pos
    )
    expert_out = combined[row_index]
    return (gates[:, None] * expert_out).astype(jnp.bfloat16)


def solution(mesh):
    in_specs = (
        P(("rep", "ep"), None),
        P(("rep", "ep")),
        P(("rep", "ep"), None),
        P(None, "ep"),
        P("ep", None),
    )
    out_specs = P(("rep", "ep"), None)
    return jax.shard_map(body, mesh=mesh, in_specs=in_specs, out_specs=out_specs, check_vma=False)
```

profile of v0, /device:TPU:0, one launch (start us, length us, event | category | flops | bytes accessed | tf_op | source)
XLA Modules:
  0.0 149.7 jit_solution(4015990323748989319)
XLA Ops:
  1.6 1.9 %scatter_custom_fusion.1 = bf16[65,2048]{1,0:T(8,128)(2,1)S(1)} fusion(s32[128]{0:T(128)S(1)} %get-tuple-element.10, bf16[128,2048]{1,0:T(8,128)(2,1)} %param.5, bf16[]{:T(256)} %constant.81.clone.1), kind=kCustom, calls=%fused_computation.43 | custom fusion | bytes 266752 | tf_op jit(solution)/shard_map/scatter | solution.py:50
  4.3 1.3 collective-permute-done.4
  5.6 8.2 %all-to-all-start.2 = ((bf16[16,16,512]{2,1,0:T(8,128)(2,1)}), bf16[16,16,512]{2,1,0:T(8,128)(2,1)S(1)}, u32[]{:S(2)}, u32[]{:S(2)}) async-start(bf16[16,16,512]{2,1,0:T(8,128)(2,1)} %collective-permute-done.4), calls=%async_computation.2 | async-start | bytes 524288 | tf_op jit(solution)/shard_map/all_to_all | solution.py:108
  13.8 2.0 %scatter_custom_fusion = bf16[97,2048]{1,0:T(8,128)(2,1)S(1)} fusion(s32[128]{0:T(128)S(1)} %get-tuple-element.11, bf16[128,2048]{1,0:T(8,128)(2,1)} %param.5, bf16[]{:T(256)} %constant.81.clone.1), kind=kCustom, calls=%fused_computation.41 | custom fusion | bytes 397824 | tf_op jit(solution)/shard_map/scatter | solution.py:47
  17.0 7.1 %all-to-all-done.2 = bf16[16,16,512]{2,1,0:T(8,128)(2,1)S(1)} async-done(((bf16[16,16,512]{2,1,0:T(8,128)(2,1)}), bf16[16,16,512]{2,1,0:T(8,128)(2,1)S(1)}, u32[]{:S(2)}, u32[]{:S(2)}) %all-to-all-start.2) | async-done | bytes 262176 | tf_op jit(solution)/shard_map/all_to_all | solution.py:108
  24.0 3.7 %all-to-all-start = ((bf16[16,24,512]{2,1,0:T(8,128)(2,1)}), bf16[16,24,512]{2,1,0:T(8,128)(2,1)S(1)}, u32[]{:S(2)}, u32[]{:S(2)}) async-start(bf16[16,24,512]{2,1,0:T(8,128)(2,1)} %bitcast.4), calls=%async_computation | async-start | bytes 786432 | tf_op jit(solution)/shard_map/all_to_all | solution.py:96
  27.8 1.8 %collective-permute-start.5 = (bf16[16,16,512]{2,1,0:T(8,128)(2,1)S(1)}, bf16[16,16,512]{2,1,0:T(8,128)(2,1)S(1)}, u32[]{:S(2)}, u32[]{:S(2)}) collective-permute-start(bf16[16,16,512]{2,1,0:T(8,128)(2,1)S(1)} %all-to-all-done.2), channel_id=1, source_target_pairs={{0,1},{1,0},{2,3},{3,2},{4,5},{5,4},{6,7},{7,6},{8,9},{9,8},{10,11... | collective-permute-start | bytes 786440 | tf_op jit(solution)/shard_map/ppermute | solution.py:16
  29.6 10.3 %all-to-all-done = bf16[16,24,512]{2,1,0:T(8,128)(2,1)S(1)} async-done(((bf16[16,24,512]{2,1,0:T(8,128)(2,1)}), bf16[16,24,512]{2,1,0:T(8,128)(2,1)S(1)}, u32[]{:S(2)}, u32[]{:S(2)}) %all-to-all-start) | async-done | bytes 393248 | tf_op jit(solution)/shard_map/all_to_all | solution.py:96
  41.5 6.2 %collective-permute-done = bf16[16,24,512]{2,1,0:T(8,128)(2,1)S(1)} collective-permute-done((bf16[16,24,512]{2,1,0:T(8,128)(2,1)S(1)}, bf16[16,24,512]{2,1,0:T(8,128)(2,1)S(1)}, u32[]{:S(2)}, u32[]{:S(2)}) %collective-permute-start) | collective-permute-done | bytes 393248 | tf_op jit(solution)/shard_map/ppermute | solution.py:16
  48.7 1.5 collective-permute-start.1
  50.3 5.0 %collective-permute-done.6 = bf16[16,16,2,512]{3,1,0,2:T(8,128)(2,1)S(1)} collective-permute-done((bf16[16,16,2,512]{3,1,0,2:T(8,128)(2,1)S(1)}, bf16[16,16,2,512]{3,1,0,2:T(8,128)(2,1)S(1)}, u32[]{:S(2)}, u32[]{:S(2)}) %collective-permute-start.6) | collective-permute-done | bytes 524320 | tf_op jit(solution)/shard_map/ppermute | solution.py:16
  57.4 6.8 %convolution_convert_fusion.1 = bf16[256,2048]{1,0:T(8,128)(2,1)} fusion(bf16[1024,2048]{1,0:T(8,128)(2,1)} %param.9, bf16[256,2048]{1,0:T(8,128)(2,1)S(1)} %select_n.161, bf16[2048,1024]{1,0:T(8,128)(2,1)} %param.8), kind=kOutput, calls=%fused_computation.4 | convolution fusion | flops 2148532224 | bytes 10485760 | tf_op jit(solution)/shard_map/dot_general | solution.py:25
  64.2 1.8 %reshape_reshape.9 = bf16[16,16,2,2,512]{4,3,2,1,0:T(2,128)(2,1)S(1)} reshape(bf16[256,2048]{1,0:T(8,128)(2,1)} %convolution_convert_fusion.1) | data formatting | bytes 2097152 | tf_op jit(solution)/shard_map/reshape;reshape | solution.py:81
  66.0 1.5 %constant_dynamic-slice_fusion = (bf16[16,16,1,2,512]{4,3,2,1,0:T(2,128)(2,1)S(1)}, bf16[16,16,1,2,512]{4,3,2,1,0:T(2,128)(2,1)}) fusion(bf16[16,16,2,2,512]{4,3,2,1,0:T(2,128)(2,1)S(1)} %reshape_reshape.9, s32[]{:T(128)S(6)} %select_n.150, s32[]{:T(128)S(6)} %select_n.149), kind=kLoop, calls=%fused_computation.49 | loop fusion | bytes 2097160 | tf_op jit(solution)/shard_map/jit(dynamic_index_in_dim)/dynamic_slice | solution.py:83
  68.4 3.9 %collective-permute-done.1 = bf16[16,24,2,512]{3,1,0,2:T(8,128)(2,1)} collective-permute-done((bf16[16,24,2,512]{3,1,0,2:T(8,128)(2,1)}, bf16[16,24,2,512]{3,1,0,2:T(8,128)(2,1)}, u32[]{:S(2)}, u32[]{:S(2)}) %collective-permute-start.1) | collective-permute-done | bytes 786464 | tf_op jit(solution)/shard_map/ppermute | solution.py:16
  72.3 1.6 %maximum_select_fusion = bf16[16,24,2,2,512]{4,1,0,3,2:T(8,128)(2,1)S(1)} fusion(bf16[16,24,1,2,512]{4,1,0,3,2:T(8,128)(2,1)} %bitcast.9, bf16[16,24,1,2,512]{4,1,0,3,2:T(8,128)(2,1)S(1)} %maximum_select_fusion.2, pred[]{:T(512)S(6)} %eq.26), kind=kLoop, calls=%fused_computation.9 | loop fusion | flops 2359296 | bytes 3145729 | tf_op jit(solution)/shard_map/jit(_where)/select_n | solution.py:75
  73.9 1.6 %copy.27 = bf16[16,24,2,2,512]{4,3,2,1,0:T(2,128)(2,1)S(1)} copy(bf16[16,24,2,2,512]{4,1,0,3,2:T(8,128)(2,1)S(1)} %maximum_select_fusion) | data formatting | bytes 3145728 | tf_op jit(solution)/shard_map/jit(_where)/select_n | solution.py:75
  75.5 2.4 %select_n.148 = bf16[384,2048]{1,0:T(8,128)(2,1)} reshape(bf16[16,24,2,2,512]{4,3,2,1,0:T(2,128)(2,1)S(1)} %copy.27) | data formatting | bytes 3145728 | tf_op jit(solution)/shard_map/jit(_where)/select_n | solution.py:75
  77.9 8.5 %convolution_convert_fusion = bf16[384,2048]{1,0:T(8,128)(2,1)} fusion(bf16[1024,2048]{1,0:T(8,128)(2,1)} %param.9, bf16[384,2048]{1,0:T(8,128)(2,1)} %select_n.148, bf16[2048,1024]{1,0:T(8,128)(2,1)} %param.8), kind=kOutput, calls=%fused_computation.3 | convolution fusion | flops 3222798336 | bytes 11534336 | tf_op jit(solution)/shard_map/dot_general | solution.py:25
  86.4 3.1 %reshape_reshape.8 = bf16[16,24,2,2,512]{4,3,2,1,0:T(2,128)(2,1)S(1)} reshape(bf16[384,2048]{1,0:T(8,128)(2,1)} %convolution_convert_fusion) | data formatting | bytes 3145728 | tf_op jit(solution)/shard_map/reshape;reshape | solution.py:81
  89.5 1.1 constant_dynamic-slice_fusion.2
  92.7 1.9 %collective-permute-start.8 = (bf16[2,16,16,512]{3,2,1,0:T(8,128)(2,1)}, bf16[2,16,16,512]{3,2,1,0:T(8,128)(2,1)}, u32[]{:S(2)}, u32[]{:S(2)}) collective-permute-start(bf16[2,16,16,512]{3,2,1,0:T(8,128)(2,1)} %fusion.5), channel_id=1, source_target_pairs={{0,1},{1,0},{2,3},{3,2},{4,5},{5,4},{6,7},{7,6},{8,9},{9,8},{10,11... | collective-permute-start | bytes 1572872 | tf_op jit(solution)/shard_map/ppermute | solution.py:16
  94.7 9.7 %collective-permute-done.2 = bf16[16,24,2,512]{3,1,0,2:T(8,128)(2,1)S(1)} collective-permute-done((bf16[16,24,2,512]{3,1,0,2:T(8,128)(2,1)}, bf16[16,24,2,512]{3,1,0,2:T(8,128)(2,1)S(1)}, u32[]{:S(2)}, u32[]{:S(2)}) %collective-permute-start.2) | collective-permute-done | bytes 786464 | tf_op jit(solution)/shard_map/ppermute | solution.py:16
  105.3 1.6 %collective-permute-start.3 = (bf16[2,16,24,512]{3,2,1,0:T(8,128)(2,1)}, bf16[2,16,24,512]{3,2,1,0:T(8,128)(2,1)}, u32[]{:S(2)}, u32[]{:S(2)}) collective-permute-start(bf16[2,16,24,512]{3,2,1,0:T(8,128)(2,1)} %fusion.2), channel_id=1, source_target_pairs={{0,1},{1,0},{2,3},{3,2},{4,5},{5,4},{6,7},{7,6},{8,9},{9,8},{10,11... | collective-permute-start | bytes 2359304 | tf_op jit(solution)/shard_map/ppermute | solution.py:16
  107.0 1.2 convert_reduce_fusion.2
  109.0 7.0 %all-to-all-start.3 = ((bf16[16,16,512]{2,1,0:T(8,128)(2,1)}), bf16[16,16,512]{2,1,0:T(8,128)(2,1)S(1)}, u32[]{:S(2)}, u32[]{:S(2)}) async-start(bf16[16,16,512]{2,1,0:T(8,128)(2,1)} %add_convert_fusion), calls=%async_computation.3 | async-start | bytes 524288 | tf_op jit(solution)/shard_map/all_to_all | solution.py:113
  116.1 4.4 %collective-permute-done.3 = bf16[2,16,24,512]{3,2,1,0:T(8,128)(2,1)} collective-permute-done((bf16[2,16,24,512]{3,2,1,0:T(8,128)(2,1)}, bf16[2,16,24,512]{3,2,1,0:T(8,128)(2,1)}, u32[]{:S(2)}, u32[]{:S(2)}) %collective-permute-start.3) | collective-permute-done | bytes 786464 | tf_op jit(solution)/shard_map/ppermute | solution.py:16
  120.5 1.3 convert_reduce_fusion
  122.9 1.6 %all-to-all-done.3 = bf16[16,16,512]{2,1,0:T(8,128)(2,1)S(1)} async-done(((bf16[16,16,512]{2,1,0:T(8,128)(2,1)}), bf16[16,16,512]{2,1,0:T(8,128)(2,1)S(1)}, u32[]{:S(2)}, u32[]{:S(2)}) %all-to-all-start.3) | async-done | bytes 262176 | tf_op jit(solution)/shard_map/all_to_all | solution.py:113
  124.5 8.4 %all-to-all-start.1 = ((f32[16,24,512]{2,1,0:T(8,128)}), f32[16,24,512]{2,1,0:T(8,128)S(1)}, u32[]{:S(2)}, u32[]{:S(2)}) async-start(f32[16,24,512]{2,1,0:T(8,128)} %add.95), calls=%async_computation.1 | async-start | bytes 1572864 | tf_op jit(solution)/shard_map/all_to_all | solution.py:104
  133.0 1.5 %collective-permute-done.9 = bf16[16,16,512]{2,1,0:T(8,128)(2,1)S(1)} collective-permute-done((bf16[16,16,512]{2,1,0:T(8,128)(2,1)S(1)}, bf16[16,16,512]{2,1,0:T(8,128)(2,1)S(1)}, u32[]{:S(2)}, u32[]{:S(2)}) %collective-permute-start.9) | collective-permute-done | bytes 262176 | tf_op jit(solution)/shard_map/ppermute | solution.py:16
  135.1 11.9 %all-to-all-done.1 = f32[16,24,512]{2,1,0:T(8,128)S(1)} async-done(((f32[16,24,512]{2,1,0:T(8,128)}), f32[16,24,512]{2,1,0:T(8,128)S(1)}, u32[]{:S(2)}, u32[]{:S(2)}) %all-to-all-start.1) | async-done | bytes 786464 | tf_op jit(solution)/shard_map/all_to_all | solution.py:104
  (47 shorter events, 17.8 us)
Async XLA Ops:
  3.8 1.9 %collective-permute-start.4 = (bf16[16,16,512]{2,1,0:T(8,128)(2,1)S(1)}, bf16[16,16,512]{2,1,0:T(8,128)(2,1)}, u32[]{:S(2)}, u32[]{:S(2)}) collective-permute-start(bf16[16,16,512]{2,1,0:T(8,128)(2,1)S(1)} %bitcast.98), channel_id=1, source_target_pairs={{0,16},{16,0},{1,17},{17,1},{2,18},{18,2},{3,19},{19,3},{4,20},{20... | collective-permute-start | bytes 786440 | tf_op jit(solution)/shard_map/ppermute | solution.py:16
  5.6 18.4 %all-to-all-start.2 = ((bf16[16,16,512]{2,1,0:T(8,128)(2,1)}), bf16[16,16,512]{2,1,0:T(8,128)(2,1)S(1)}, u32[]{:S(2)}, u32[]{:S(2)}) async-start(bf16[16,16,512]{2,1,0:T(8,128)(2,1)} %collective-permute-done.4), calls=%async_computation.2 | async-start | bytes 524288 | tf_op jit(solution)/shard_map/all_to_all | solution.py:108
  24.0 15.8 %all-to-all-start = ((bf16[16,24,512]{2,1,0:T(8,128)(2,1)}), bf16[16,24,512]{2,1,0:T(8,128)(2,1)S(1)}, u32[]{:S(2)}, u32[]{:S(2)}) async-start(bf16[16,24,512]{2,1,0:T(8,128)(2,1)} %bitcast.4), calls=%async_computation | async-start | bytes 786432 | tf_op jit(solution)/shard_map/all_to_all | solution.py:96
  27.8 12.6 %collective-permute-start.5 = (bf16[16,16,512]{2,1,0:T(8,128)(2,1)S(1)}, bf16[16,16,512]{2,1,0:T(8,128)(2,1)S(1)}, u32[]{:S(2)}, u32[]{:S(2)}) collective-permute-start(bf16[16,16,512]{2,1,0:T(8,128)(2,1)S(1)} %all-to-all-done.2), channel_id=1, source_target_pairs={{0,1},{1,0},{2,3},{3,2},{4,5},{5,4},{6,7},{7,6},{8,9},{9,8},{10,11... | collective-permute-start | bytes 786440 | tf_op jit(solution)/shard_map/ppermute | solution.py:16
  39.8 7.8 %collective-permute-start = (bf16[16,24,512]{2,1,0:T(8,128)(2,1)S(1)}, bf16[16,24,512]{2,1,0:T(8,128)(2,1)S(1)}, u32[]{:S(2)}, u32[]{:S(2)}) collective-permute-start(bf16[16,24,512]{2,1,0:T(8,128)(2,1)S(1)} %all-to-all-done), channel_id=1, source_target_pairs={{0,1},{1,0},{2,3},{3,2},{4,5},{5,4},{6,7},{7,6},{8,9},{9,8},{10,11... | collective-permute-start | bytes 1179656 | tf_op jit(solution)/shard_map/ppermute | solution.py:16
  40.5 14.9 %collective-permute-start.6 = (bf16[16,16,2,512]{3,1,0,2:T(8,128)(2,1)S(1)}, bf16[16,16,2,512]{3,1,0,2:T(8,128)(2,1)S(1)}, u32[]{:S(2)}, u32[]{:S(2)}) collective-permute-start(bf16[16,16,2,512]{3,1,0,2:T(8,128)(2,1)S(1)} %maximum_select_fusion.5), channel_id=1, source_target_pairs={{0,2},{2,0},{1,3},{3,1},{4,6},{6,4},{5,7},{7,5},{8,10},{10,8},{9,1... | collective-permute-start | bytes 1572872 | tf_op jit(solution)/shard_map/ppermute | solution.py:16
  48.7 23.6 %collective-permute-start.1 = (bf16[16,24,2,512]{3,1,0,2:T(8,128)(2,1)}, bf16[16,24,2,512]{3,1,0,2:T(8,128)(2,1)}, u32[]{:S(2)}, u32[]{:S(2)}) collective-permute-start(bf16[16,24,2,512]{3,1,0,2:T(8,128)(2,1)} %maximum_select_fusion.3), channel_id=1, source_target_pairs={{0,2},{2,0},{1,3},{3,1},{4,6},{6,4},{5,7},{7,5},{8,10},{10,8},{9,1... | collective-permute-start | bytes 2359304 | tf_op jit(solution)/shard_map/ppermute | solution.py:16
  68.4 23.4 %collective-permute-start.7 = (bf16[16,16,2,512]{3,1,0,2:T(8,128)(2,1)}, bf16[16,16,2,512]{3,1,0,2:T(8,128)(2,1)S(1)}, u32[]{:S(2)}, u32[]{:S(2)}) collective-permute-start(bf16[16,16,2,512]{3,1,0,2:T(8,128)(2,1)} %bitcast.71), channel_id=1, source_target_pairs={{0,2},{2,0},{1,3},{3,1},{4,6},{6,4},{5,7},{7,5},{8,10},{10,8},{9,1... | collective-permute-start | bytes 1572872 | tf_op jit(solution)/shard_map/ppermute | solution.py:16
  90.6 1.2 copy-start
  91.6 12.8 %collective-permute-start.2 = (bf16[16,24,2,512]{3,1,0,2:T(8,128)(2,1)}, bf16[16,24,2,512]{3,1,0,2:T(8,128)(2,1)S(1)}, u32[]{:S(2)}, u32[]{:S(2)}) collective-permute-start(bf16[16,24,2,512]{3,1,0,2:T(8,128)(2,1)} %bitcast.69), channel_id=1, source_target_pairs={{0,2},{2,0},{1,3},{3,1},{4,6},{6,4},{5,7},{7,5},{8,10},{10,8},{9,1... | collective-permute-start | bytes 2359304 | tf_op jit(solution)/shard_map/ppermute | solution.py:16
  92.7 14.3 %collective-permute-start.8 = (bf16[2,16,16,512]{3,2,1,0:T(8,128)(2,1)}, bf16[2,16,16,512]{3,2,1,0:T(8,128)(2,1)}, u32[]{:S(2)}, u32[]{:S(2)}) collective-permute-start(bf16[2,16,16,512]{3,2,1,0:T(8,128)(2,1)} %fusion.5), channel_id=1, source_target_pairs={{0,1},{1,0},{2,3},{3,2},{4,5},{5,4},{6,7},{7,6},{8,9},{9,8},{10,11... | collective-permute-start | bytes 1572872 | tf_op jit(solution)/shard_map/ppermute | solution.py:16
  105.3 15.1 %collective-permute-start.3 = (bf16[2,16,24,512]{3,2,1,0:T(8,128)(2,1)}, bf16[2,16,24,512]{3,2,1,0:T(8,128)(2,1)}, u32[]{:S(2)}, u32[]{:S(2)}) collective-permute-start(bf16[2,16,24,512]{3,2,1,0:T(8,128)(2,1)} %fusion.2), channel_id=1, source_target_pairs={{0,1},{1,0},{2,3},{3,2},{4,5},{5,4},{6,7},{7,6},{8,9},{9,8},{10,11... | collective-permute-start | bytes 2359304 | tf_op jit(solution)/shard_map/ppermute | solution.py:16
  109.0 15.5 %all-to-all-start.3 = ((bf16[16,16,512]{2,1,0:T(8,128)(2,1)}), bf16[16,16,512]{2,1,0:T(8,128)(2,1)S(1)}, u32[]{:S(2)}, u32[]{:S(2)}) async-start(bf16[16,16,512]{2,1,0:T(8,128)(2,1)} %add_convert_fusion), calls=%async_computation.3 | async-start | bytes 524288 | tf_op jit(solution)/shard_map/all_to_all | solution.py:113
  124.5 22.5 %all-to-all-start.1 = ((f32[16,24,512]{2,1,0:T(8,128)}), f32[16,24,512]{2,1,0:T(8,128)S(1)}, u32[]{:S(2)}, u32[]{:S(2)}) async-start(f32[16,24,512]{2,1,0:T(8,128)} %add.95), calls=%async_computation.1 | async-start | bytes 1572864 | tf_op jit(solution)/shard_map/all_to_all | solution.py:104
  132.9 1.6 %collective-permute-start.9 = (bf16[16,16,512]{2,1,0:T(8,128)(2,1)S(1)}, bf16[16,16,512]{2,1,0:T(8,128)(2,1)S(1)}, u32[]{:S(2)}, u32[]{:S(2)}) collective-permute-start(bf16[16,16,512]{2,1,0:T(8,128)(2,1)S(1)} %all-to-all-done.3), channel_id=1, source_target_pairs={{0,16},{16,0},{1,17},{17,1},{2,18},{18,2},{3,19},{19,3},{4,20},{20... | collective-permute-start | bytes 786440 | tf_op jit(solution)/shard_map/ppermute | solution.py:16
  147.8 1.0 copy-start.1
where the time goes:
time: 151 us; the launch traced here: 150 us
  waiting for transfers between devices  62.7 us (42%)
  starting transfers between devices  36.2 us (24%)
  local copies, waits for them, and re-layouts  23.1 us (15%)
  matrix products  15.3 us (10%)
  other arithmetic  12.1 us (8%)
    ppermute x10, waiting for transfers between devices, from_partner(): return lax.ppermute(block, axis, route)  31.9 us
    dot_general x2, matrix products, feed(): jnp.dot(hidden, weight_out, preferred_element_type=jnp.float32)  15.3 us
    all_to_all x1, waiting for transfers between devices, body(): lax.all_to_all(summed, 'ep', split_axis=0, concat_axis=0, tiled=True)  11.9 us
    all_to_all x1, waiting for transfers between devices, body(): lax.all_to_all(narrow(main_buffer, capacity), 'ep', split_axis=0, concat_...  10.3 us
    ppermute x10, starting transfers between devices, from_partner(): return lax.ppermute(block, axis, route)  8.86 us
    all_to_all x1, starting transfers between devices, body(): lax.all_to_all(summed, 'ep', split_axis=0, concat_axis=0, tiled=True)  8.43 us
    all_to_all x1, starting transfers between devices, body(): lax.all_to_all(moved_rows, 'ep', split_axis=0, concat_axis=0, tiled=True)  8.22 us
    all_to_all x1, waiting for transfers between devices, body(): lax.all_to_all(moved_rows, 'ep', split_axis=0, concat_axis=0, tiled=True)  7.06 us
  transfers between devices with their start and end apart: 14, of which 11 were waited for; matrix products, arithmetic and copies ran while one was open for 29% of the time, Pallas kernels for 0%

commit v1 on v0

v1 whole, which is shorter than its diff:
```python
import functools

import jax
import jax.numpy as jnp
from jax import lax
from jax.experimental import pallas as pl
from jax.experimental.pallas import tpu as pltpu
from jax.sharding import PartitionSpec as P

SLICES = 4
AXES = ("rep", "ep")


def route(partner):
    reps, owners = lax.axis_size("rep"), lax.axis_size("ep")
    pairs = []
    for rep in range(reps):
        for ep in range(owners):
            to_rep, to_ep = partner(rep, ep)
            pairs.append((rep * owners + ep, to_rep * owners + to_ep))
    return pairs


def slots_row(ids_ref, here_ref, experts, seats):
    count = ids_ref.shape[1]
    distance = ids_ref[...] ^ here_ref[0]
    named = (lax.broadcasted_iota(jnp.int32, (experts, count), 0) == distance).astype(jnp.bfloat16)
    earlier = (
        lax.broadcasted_iota(jnp.int32, (count, count), 0)
        < lax.broadcasted_iota(jnp.int32, (count, count), 1)
    ).astype(jnp.bfloat16)
    ahead = jnp.dot(named, earlier, preferred_element_type=jnp.float32)
    rank = jnp.sum(named.astype(jnp.float32) * ahead, axis=0, keepdims=True)
    return distance.astype(jnp.float32) * seats + rank


def pack_kernel(experts, seats, here_ref, ids_ref, tokens_ref, *out_refs):
    count = ids_ref.shape[1]
    slot = slots_row(ids_ref, here_ref, experts, seats).astype(jnp.int32)
    chosen = lax.broadcasted_iota(jnp.int32, (experts * seats, count), 0) == slot
    rows = jnp.dot(
        chosen.astype(jnp.bfloat16), tokens_ref[...], preferred_element_type=jnp.float32
    ).astype(jnp.bfloat16)
    for index, ref in enumerate(out_refs):
        ref[...] = rows[index * seats : (index + 1) * seats]


def unpack_kernel(experts, seats, here_ref, ids_ref, gates_ref, *refs):
    out_ref = refs[-1]
    count = ids_ref.shape[1]
    slot = slots_row(ids_ref, here_ref, experts, seats)
    same = lax.broadcasted_iota(jnp.int32, (count, count), 0) == lax.broadcasted_iota(
        jnp.int32, (count, count), 1
    )
    slot = jnp.sum(jnp.where(same, slot, 0.0), axis=1, keepdims=True).astype(jnp.int32)
    gate = jnp.sum(jnp.where(same, gates_ref[...], 0.0), axis=1, keepdims=True)
    lane = lax.broadcasted_iota(jnp.int32, (count, seats), 1)
    total = jnp.zeros(out_ref.shape, jnp.float32)
    for index, ref in enumerate(refs[:-1]):
        chosen = (slot - index * seats == lane).astype(jnp.bfloat16)
        total = total + jnp.dot(chosen, ref[...], preferred_element_type=jnp.float32)
    out_ref[...] = (total * gate).astype(jnp.bfloat16)


def feed_kernel(rows_ref, weight_in_ref, weight_out_ref, out_ref, hidden_ref):
    inner = weight_in_ref.shape[1]
    width = weight_out_ref.shape[1]
    block = 256

    def first(step, carry):
        columns = pl.ds(pl.multiple_of(step * block, block), block)
        hidden = jnp.dot(
            rows_ref[...], weight_in_ref[:, columns], preferred_element_type=jnp.float32
        )
        hidden_ref[:, columns] = jnp.maximum(hidden, 0.0).astype(jnp.bfloat16)
        return carry

    lax.fori_loop(0, inner // block, first, 0)

    def second(step, carry):
        columns = pl.ds(pl.multiple_of(step * block, block), block)
        out_ref[:, columns] = jnp.dot(
            hidden_ref[...], weight_out_ref[:, columns], preferred_element_type=jnp.float32
        ).astype(jnp.bfloat16)
        return carry

    lax.fori_loop(0, width // block, second, 0)


def feed(rows, weight_in, weight_out):
    count, width = rows.shape
    inner = weight_in.shape[1]
    vmem = pl.BlockSpec(memory_space=pltpu.VMEM)
    return pl.pallas_call(
        feed_kernel,
        out_shape=jax.ShapeDtypeStruct((count, width), jnp.bfloat16),
        in_specs=[vmem] * 3,
        out_specs=vmem,
        scratch_shapes=[pltpu.VMEM((count, inner), jnp.bfloat16)],
        compiler_params=pltpu.CompilerParams(vmem_limit_bytes=24 * 2**20),
        cost_estimate=pl.CostEstimate(
            flops=4 * count * width * inner, bytes_accessed=4 * width * inner, transcendentals=0
        ),
    )(rows, weight_in, weight_out)


def chunks_of(experts):
    if experts == 4:
        return ((0, 1), (3,), (2,))
    half = experts // 2
    return (tuple(range(half)), tuple(range(half, experts)))


def body(tokens, gates, expert_ids, weight_in, weight_out):
    owner_count = lax.axis_size("ep")
    experts = owner_count // SLICES
    tok_rows, width = tokens.shape
    bound = 3 * tok_rows // (4 * experts) + tok_rows // (2 * experts)
    seats = -(-bound // 8) * 8
    here = (lax.axis_index("ep") // SLICES).astype(jnp.int32).reshape(1)
    ids = expert_ids.reshape(1, tok_rows)
    smem = pl.BlockSpec(memory_space=pltpu.SMEM)
    vmem = pl.BlockSpec(memory_space=pltpu.VMEM)

    near = route(lambda rep, ep: (rep, ep ^ (1 if rep % 2 == 0 else 2)))
    far = route(lambda rep, ep: (rep, ep ^ (2 if rep % 2 == 0 else 1)))

    def across(block, distance):
        if distance == 0:
            return block
        return lax.ppermute(block, AXES, route(lambda rep, ep: (rep, ep ^ (SLICES * distance))))

    packed = pl.pallas_call(
        functools.partial(pack_kernel, experts, seats),
        out_shape=[jax.ShapeDtypeStruct((seats, width), jnp.bfloat16)] * experts,
        in_specs=[smem, vmem, vmem],
        out_specs=[vmem] * experts,
    )(here, ids, tokens)

    groups = chunks_of(experts)
    done = [None] * experts
    for group in groups:
        parts = [across(packed[distance], distance) for distance in group]
        mine = parts[0] if len(parts) == 1 else jnp.concatenate(parts, axis=0)
        count = mine.shape[0]
        pair = jnp.concatenate([mine, lax.ppermute(mine, AXES, near)], axis=0)
        other = lax.ppermute(pair, AXES, far)
        give = feed(other, weight_in, weight_out)
        keep = feed(pair, weight_in, weight_out)
        taken = lax.ppermute(give, AXES, far)
        both = keep.astype(jnp.float32) + taken.astype(jnp.float32)
        landed = lax.ppermute(both[count:].astype(jnp.bfloat16), AXES, near)
        total = (both[:count] + landed.astype(jnp.float32)).astype(jnp.bfloat16)
        for index, distance in enumerate(group):
            done[distance] = across(total[index * seats : (index + 1) * seats], distance)

    return pl.pallas_call(
        functools.partial(unpack_kernel, experts, seats),
        out_shape=jax.ShapeDtypeStruct((tok_rows, width), jnp.bfloat16),
        in_specs=[smem] + [vmem] * (experts + 2),
        out_specs=vmem,
    )(here, ids, gates.reshape(1, tok_rows), *done)


def solution(mesh):
    in_specs = (
        P(("rep", "ep"), None),
        P(("rep", "ep")),
        P(("rep", "ep"), None),
        P(None, "ep"),
        P("ep", None),
    )
    out_specs = P(("rep", "ep"), None)
    return jax.shard_map(body, mesh=mesh, in_specs=in_specs, out_specs=out_specs, check_vma=False)
```

time: 151 us -> 95.1 us (0.63)
  waiting for transfers between devices: 62.7 us -> 26.7 us
  Pallas kernels: 0 us -> 25.2 us
  local copies, waits for them, and re-layouts: 23.1 us -> 6.81 us
  matrix products: 15.3 us -> 0 us
  other arithmetic: 12.1 us -> 1.36 us
  starting transfers between devices: 36.2 us -> 34.6 us
    all_to_all x4 -> x0, waiting for transfers between devices: 30.8 us -> none  [the longest x1 11.9 us: body(): lax.all_to_all(summed, 'ep', split_axis=0, concat_axis=0, tiled=True)]
    all_to_all x4 -> x0, starting transfers between devices: 27.4 us -> none  [the longest x1 8.43 us: body(): lax.all_to_all(summed, 'ep', split_axis=0, concat_axis=0, tiled=True)]
    ppermute x10 -> x18, starting transfers between devices: 8.86 us -> 34.6 us  [the longest x6 17.8 us: across(): lax.ppermute(block, AXES, route(lambda rep, ep: (rep, ep ^ SLICES * dista...]
    pallas_call x0 -> x8, Pallas kernels: none -> 25.2 us  [the longest x6 20 us: feed(): pl.pallas_call(feed_kernel, out_shape=jax.ShapeDtypeStruct((count, width)...]
    dot_general x2 -> x0, matrix products: 15.3 us -> none  [feed(): jnp.dot(hidden, weight_out, preferred_element_type=jnp.float32)]
    select_n x4 -> x0, local copies, waits for them, and re-layouts: 5.94 us -> none  [gather_group(): jnp.where(high_bit == 0, jnp.stack([pair, across], -3), jnp.stack([across...]
    unnamed x6 -> x16, local copies, waits for them, and re-layouts: 0.6 us -> 6 us
    ppermute x10 -> x18, waiting for transfers between devices: 31.9 us -> 26.7 us  [the longest x6 10.8 us: across(): lax.ppermute(block, AXES, route(lambda rep, ep: (rep, ep ^ SLICES * dista...]
  transfers between devices with their start and end apart: 14 -> 18, of which waited for: 11 -> 7; matrix products, arithmetic and copies ran while one was open for 29% -> 3% of each run, Pallas kernels for 0% -> 21%
where the time goes in v1:
time: 95.1 us; the launch traced here: 94.8 us
  starting transfers between devices  34.6 us (36%)
  waiting for transfers between devices  26.7 us (28%)
  Pallas kernels  25.2 us (26%)
  local copies, waits for them, and re-layouts  6.81 us (7%)
  other arithmetic  1.36 us (1%)
    pallas_call x6, Pallas kernels, feed(): pl.pallas_call(feed_kernel, out_shape=jax.ShapeDtypeStruct((count, width)...  20 us
    ppermute x6, starting transfers between devices, across(): lax.ppermute(block, AXES, route(lambda rep, ep: (rep, ep ^ SLICES * dista...  17.8 us
    ppermute x6, waiting for transfers between devices, across(): lax.ppermute(block, AXES, route(lambda rep, ep: (rep, ep ^ SLICES * dista...  10.8 us
    unnamed x16, local copies, waits for them, and re-layouts  6 us
    ppermute x3, waiting for transfers between devices, body(): taken = lax.ppermute(give, AXES, far)  5.18 us
    ppermute x3, starting transfers between devices, body(): pair = jnp.concatenate([mine, lax.ppermute(mine, AXES, near)], axis=0)  4.72 us
    ppermute x3, starting transfers between devices, body(): taken = lax.ppermute(give, AXES, far)  4.7 us
    ppermute x3, starting transfers between devices, body(): landed = lax.ppermute(both[count:].astype(jnp.bfloat16), AXES, near)  4.67 us
  transfers between devices with their start and end apart: 18, of which 7 were waited for; matrix products, arithmetic and copies ran while one was open for 3% of the time, Pallas kernels for 21%

profile of v1, /device:TPU:0, one launch (start us, length us, event | category | flops | bytes accessed | tf_op | source)
XLA Modules:
  0.0 94.8 jit_solution(14128899521433017305)
XLA Ops:
  0.0 2.3 %shard_map.55 = (bf16[40,2048]{1,0:T(8,128)(2,1)}, bf16[40,2048]{1,0:T(8,128)(2,1)}, bf16[40,2048]{1,0:T(8,128)(2,1)}, bf16[40,2048]{1,0:T(8,128)(2,1)}) custom-call(s32[1]{0:T(128)} %bitcast.here_ref, s32[1,128]{1,0:T(1,128)} %bitcast.3, bf16[128,2048]{1,0:T(8,128)(2,1)} %tokens_ref.1), custom_call_target="tpu_custom_call" | custom-call | tf_op jit(solution)/shard_map/pallas_call | solution.py:133
  2.3 3.1 %collective-permute-start = (bf16[40,2048]{1,0:T(8,128)(2,1)}, bf16[40,2048]{1,0:T(8,128)(2,1)S(1)}, u32[]{:S(2)}, u32[]{:S(2)}) collective-permute-start(bf16[40,2048]{1,0:T(8,128)(2,1)} %get-tuple-element.10), channel_id=1, source_target_pairs={{0,4},{1,5},{2,6},{3,7},{4,0},{5,1},{6,2},{7,3},{8,12},{9,13},{10,... | collective-permute-start | bytes 491528 | tf_op jit(solution)/shard_map/ppermute | solution.py:131
  5.3 2.6 %collective-permute-start.6 = (bf16[40,2048]{1,0:T(8,128)(2,1)}, bf16[40,2048]{1,0:T(8,128)(2,1)S(1)}, u32[]{:S(2)}, u32[]{:S(2)}) collective-permute-start(bf16[40,2048]{1,0:T(8,128)(2,1)} %get-tuple-element.11), channel_id=1, source_target_pairs={{0,8},{1,9},{2,10},{3,11},{4,12},{5,13},{6,14},{7,15},{8,0},{9,1},... | collective-permute-start | bytes 491528 | tf_op jit(solution)/shard_map/ppermute | solution.py:131
  8.9 3.4 %collective-permute-done = bf16[40,2048]{1,0:T(8,128)(2,1)S(1)} collective-permute-done((bf16[40,2048]{1,0:T(8,128)(2,1)}, bf16[40,2048]{1,0:T(8,128)(2,1)S(1)}, u32[]{:S(2)}, u32[]{:S(2)}) %collective-permute-start) | collective-permute-done | bytes 163872 | tf_op jit(solution)/shard_map/ppermute | solution.py:131
  13.2 1.8 %collective-permute-start.1 = (bf16[80,2048]{1,0:T(8,128)(2,1)S(1)}, bf16[80,2048]{1,0:T(8,128)(2,1)S(1)}, u32[]{:S(2)}, u32[]{:S(2)}) collective-permute-start(bf16[80,2048]{1,0:T(8,128)(2,1)S(1)} %pad_maximum_fusion), channel_id=1, source_target_pairs={{0,1},{1,0},{2,3},{3,2},{4,5},{5,4},{6,7},{7,6},{8,9},{9,8},{10,11... | collective-permute-start | bytes 983048 | tf_op jit(solution)/shard_map/ppermute | solution.py:146
  15.0 4.1 %collective-permute-done.12 = bf16[40,2048]{1,0:T(8,128)(2,1)S(1)} collective-permute-done((bf16[40,2048]{1,0:T(8,128)(2,1)}, bf16[40,2048]{1,0:T(8,128)(2,1)S(1)}, u32[]{:S(2)}, u32[]{:S(2)}) %collective-permute-start.12) | collective-permute-done | bytes 163872 | tf_op jit(solution)/shard_map/ppermute | solution.py:131
  19.1 1.5 %collective-permute-start.13 = (bf16[40,2048]{1,0:T(8,128)(2,1)S(1)}, bf16[40,2048]{1,0:T(8,128)(2,1)S(1)}, u32[]{:S(2)}, u32[]{:S(2)}) collective-permute-start(bf16[40,2048]{1,0:T(8,128)(2,1)S(1)} %collective-permute-done.12), channel_id=1, source_target_pairs={{0,1},{1,0},{2,3},{3,2},{4,5},{5,4},{6,7},{7,6},{8,9},{9,8},{10,11... | collective-permute-start | bytes 491528 | tf_op jit(solution)/shard_map/ppermute | solution.py:146
  20.6 1.5 %collective-permute-start.7 = (bf16[40,2048]{1,0:T(8,128)(2,1)S(1)}, bf16[40,2048]{1,0:T(8,128)(2,1)S(1)}, u32[]{:S(2)}, u32[]{:S(2)}) collective-permute-start(bf16[40,2048]{1,0:T(8,128)(2,1)S(1)} %collective-permute-done.6), channel_id=1, source_target_pairs={{0,1},{1,0},{2,3},{3,2},{4,5},{5,4},{6,7},{7,6},{8,9},{9,8},{10,11... | collective-permute-start | bytes 491528 | tf_op jit(solution)/shard_map/ppermute | solution.py:146
  22.1 4.1 %collective-permute-done.7 = bf16[40,2048]{1,0:T(8,128)(2,1)S(1)} collective-permute-done((bf16[40,2048]{1,0:T(8,128)(2,1)S(1)}, bf16[40,2048]{1,0:T(8,128)(2,1)S(1)}, u32[]{:S(2)}, u32[]{:S(2)}) %collective-permute-start.7) | collective-permute-done | bytes 163872 | tf_op jit(solution)/shard_map/ppermute | solution.py:146
  26.2 1.6 %collective-permute-start.8 = (bf16[80,2048]{1,0:T(8,128)(2,1)S(1)}, bf16[80,2048]{1,0:T(8,128)(2,1)S(1)}, u32[]{:S(2)}, u32[]{:S(2)}) collective-permute-start(bf16[80,2048]{1,0:T(8,128)(2,1)S(1)} %constant_dynamic-update-slice_fusion.3.rows_ref), channel_id=1, source_target_pairs={{0,2},{1,3},{2,0},{3,1},{4,6},{5,7},{6,4},{7,5},{8,10},{9,11},{10,... | collective-permute-start | bytes 983048 | tf_op jit(solution)/shard_map/ppermute | solution.py:147
  28.3 2.2 %copy-done = bf16[2048,1024]{1,0:T(8,128)(2,1)S(1)} copy-done((bf16[2048,1024]{1,0:T(8,128)(2,1)S(1)}, bf16[2048,1024]{1,0:T(8,128)(2,1)}, u32[]{:S(2)}) %copy-start) | copy-done | bytes 4194328
  30.5 2.2 %copy-done.2 = bf16[1024,2048]{1,0:T(8,128)(2,1)S(1)} copy-done((bf16[1024,2048]{1,0:T(8,128)(2,1)S(1)}, bf16[1024,2048]{1,0:T(8,128)(2,1)}, u32[]{:S(2)}) %copy-start.2) | copy-done | bytes 4194328
  32.7 3.2 %shard_map.60 = bf16[80,2048]{1,0:T(8,128)(2,1)S(1)} custom-call(bf16[80,2048]{1,0:T(8,128)(2,1)S(1)} %constant_dynamic-update-slice_fusion.5.rows_ref, bf16[2048,1024]{1,0:T(8,128)(2,1)S(1)} %copy-done, bf16[1024,2048]{1,0:T(8,128)(2,1)S(1)} %copy-done.2), custom_call_target="tpu_custom_call" | custom-call | flops 671088640 | bytes 8388608 | tf_op jit(solution)/shard_map/pallas_call | solution.py:94
  35.9 3.2 %shard_map.58 = bf16[80,2048]{1,0:T(8,128)(2,1)S(1)} custom-call(bf16[80,2048]{1,0:T(8,128)(2,1)S(1)} %constant_dynamic-update-slice_fusion.3.rows_ref, bf16[2048,1024]{1,0:T(8,128)(2,1)S(1)} %copy-done, bf16[1024,2048]{1,0:T(8,128)(2,1)S(1)} %copy-done.2), custom_call_target="tpu_custom_call" | custom-call | flops 671088640 | bytes 8388608 | tf_op jit(solution)/shard_map/pallas_call | solution.py:94
  39.1 3.2 %shard_map.59 = bf16[80,2048]{1,0:T(8,128)(2,1)S(1)} custom-call(bf16[80,2048]{1,0:T(8,128)(2,1)S(1)} %collective-permute-done.8.rows_ref, bf16[2048,1024]{1,0:T(8,128)(2,1)S(1)} %copy-done, bf16[1024,2048]{1,0:T(8,128)(2,1)S(1)} %copy-done.2), custom_call_target="tpu_custom_call" | custom-call | flops 671088640 | bytes 8388608 | tf_op jit(solution)/shard_map/pallas_call | solution.py:94
  42.3 1.6 %collective-permute-start.9 = (bf16[80,2048]{1,0:T(8,128)(2,1)S(1)}, bf16[80,2048]{1,0:T(8,128)(2,1)S(1)}, u32[]{:S(2)}, u32[]{:S(2)}) collective-permute-start(bf16[80,2048]{1,0:T(8,128)(2,1)S(1)} %shard_map.59), channel_id=1, source_target_pairs={{0,2},{1,3},{2,0},{3,1},{4,6},{5,7},{6,4},{7,5},{8,10},{9,11},{10,... | collective-permute-start | bytes 983048 | tf_op jit(solution)/shard_map/ppermute | solution.py:150
  44.5 3.6 %shard_map.56 = bf16[160,2048]{1,0:T(8,128)(2,1)S(1)} custom-call(bf16[160,2048]{1,0:T(8,128)(2,1)S(1)} %constant_dynamic-update-slice_fusion.rows_ref, bf16[2048,1024]{1,0:T(8,128)(2,1)S(1)} %copy-done, bf16[1024,2048]{1,0:T(8,128)(2,1)S(1)} %copy-done.2), custom_call_target="tpu_custom_call" | custom-call | flops 1342177280 | bytes 8388608 | tf_op jit(solution)/shard_map/pallas_call | solution.py:94
  48.1 3.2 %shard_map.61 = bf16[80,2048]{1,0:T(8,128)(2,1)S(1)} custom-call(bf16[80,2048]{1,0:T(8,128)(2,1)S(1)} %collective-permute-done.14.rows_ref, bf16[2048,1024]{1,0:T(8,128)(2,1)S(1)} %copy-done, bf16[1024,2048]{1,0:T(8,128)(2,1)S(1)} %copy-done.2), custom_call_target="tpu_custom_call" | custom-call | flops 671088640 | bytes 8388608 | tf_op jit(solution)/shard_map/pallas_call | solution.py:94
  51.3 1.6 %collective-permute-start.15 = (bf16[80,2048]{1,0:T(8,128)(2,1)S(1)}, bf16[80,2048]{1,0:T(8,128)(2,1)S(1)}, u32[]{:S(2)}, u32[]{:S(2)}) collective-permute-start(bf16[80,2048]{1,0:T(8,128)(2,1)S(1)} %shard_map.61), channel_id=1, source_target_pairs={{0,2},{1,3},{2,0},{3,1},{4,6},{5,7},{6,4},{7,5},{8,10},{9,11},{10,... | collective-permute-start | bytes 983048 | tf_op jit(solution)/shard_map/ppermute | solution.py:150
  53.0 1.6 %collective-permute-start.10 = (bf16[40,2048]{1,0:T(8,128)(2,1)S(1)}, bf16[40,2048]{1,0:T(8,128)(2,1)S(1)}, u32[]{:S(2)}, u32[]{:S(2)}) collective-permute-start(bf16[40,2048]{1,0:T(8,128)(2,1)S(1)} %slice.57), channel_id=1, source_target_pairs={{0,1},{1,0},{2,3},{3,2},{4,5},{5,4},{6,7},{7,6},{8,9},{9,8},{10,11... | collective-permute-start | bytes 491528 | tf_op jit(solution)/shard_map/ppermute | solution.py:152
  54.5 3.6 %collective-permute-done.2.rows_ref = bf16[160,2048]{1,0:T(8,128)(2,1)S(1)} collective-permute-done((bf16[160,2048]{1,0:T(8,128)(2,1)S(1)}, bf16[160,2048]{1,0:T(8,128)(2,1)S(1)}, u32[]{:S(2)}, u32[]{:S(2)}) %collective-permute-start.2) | collective-permute-done | bytes 655392 | tf_op jit(solution)/shard_map/ppermute | solution.py:147
  58.2 3.6 %shard_map.57 = bf16[160,2048]{1,0:T(8,128)(2,1)S(1)} custom-call(bf16[160,2048]{1,0:T(8,128)(2,1)S(1)} %collective-permute-done.2.rows_ref, bf16[2048,1024]{1,0:T(8,128)(2,1)S(1)} %copy-done.1, bf16[1024,2048]{1,0:T(8,128)(2,1)S(1)} %copy-done.2), custom_call_target="tpu_custom_call" | custom-call | flops 1342177280 | bytes 8388608 | tf_op jit(solution)/shard_map/pallas_call | solution.py:94
  61.8 1.6 %collective-permute-start.3 = (bf16[160,2048]{1,0:T(8,128)(2,1)S(1)}, bf16[160,2048]{1,0:T(8,128)(2,1)S(1)}, u32[]{:S(2)}, u32[]{:S(2)}) collective-permute-start(bf16[160,2048]{1,0:T(8,128)(2,1)S(1)} %shard_map.57), channel_id=1, source_target_pairs={{0,2},{1,3},{2,0},{3,1},{4,6},{5,7},{6,4},{7,5},{8,10},{9,11},{10,... | collective-permute-start | bytes 1966088 | tf_op jit(solution)/shard_map/ppermute | solution.py:150
  63.5 1.6 %collective-permute-start.16 = (bf16[40,2048]{1,0:T(8,128)(2,1)S(1)}, bf16[40,2048]{1,0:T(8,128)(2,1)S(1)}, u32[]{:S(2)}, u32[]{:S(2)}) collective-permute-start(bf16[40,2048]{1,0:T(8,128)(2,1)S(1)} %slice.56), channel_id=1, source_target_pairs={{0,1},{1,0},{2,3},{3,2},{4,5},{5,4},{6,7},{7,6},{8,9},{9,8},{10,11... | collective-permute-start | bytes 491528 | tf_op jit(solution)/shard_map/ppermute | solution.py:152
  65.1 5.3 %collective-permute-start.11 = (bf16[40,2048]{1,0:T(8,128)(2,1)S(1)}, bf16[40,2048]{1,0:T(8,128)(2,1)S(1)}, u32[]{:S(2)}, u32[]{:S(2)}) collective-permute-start(bf16[40,2048]{1,0:T(8,128)(2,1)S(1)} %fusion.2), channel_id=1, source_target_pairs={{0,8},{1,9},{2,10},{3,11},{4,12},{5,13},{6,14},{7,15},{8,0},{9,1},... | collective-permute-start | bytes 491528 | tf_op jit(solution)/shard_map/ppermute | solution.py:131
  70.4 5.2 %collective-permute-done.3 = bf16[160,2048]{1,0:T(8,128)(2,1)S(1)} collective-permute-done((bf16[160,2048]{1,0:T(8,128)(2,1)S(1)}, bf16[160,2048]{1,0:T(8,128)(2,1)S(1)}, u32[]{:S(2)}, u32[]{:S(2)}) %collective-permute-start.3) | collective-permute-done | bytes 655392 | tf_op jit(solution)/shard_map/ppermute | solution.py:150
  75.8 1.5 %collective-permute-start.4 = (bf16[80,2048]{1,0:T(8,128)(2,1)S(1)}, bf16[80,2048]{1,0:T(8,128)(2,1)S(1)}, u32[]{:S(2)}, u32[]{:S(2)}) collective-permute-start(bf16[80,2048]{1,0:T(8,128)(2,1)S(1)} %slice.55), channel_id=1, source_target_pairs={{0,1},{1,0},{2,3},{3,2},{4,5},{5,4},{6,7},{7,6},{8,9},{9,8},{10,11... | collective-permute-start | bytes 983048 | tf_op jit(solution)/shard_map/ppermute | solution.py:152
  77.4 2.5 %collective-permute-start.17 = (bf16[40,2048]{1,0:T(8,128)(2,1)S(1)}, bf16[40,2048]{1,0:T(8,128)(2,1)S(1)}, u32[]{:S(2)}, u32[]{:S(2)}) collective-permute-start(bf16[40,2048]{1,0:T(8,128)(2,1)S(1)} %fusion.1), channel_id=1, source_target_pairs={{0,12},{1,13},{2,14},{3,15},{4,8},{5,9},{6,10},{7,11},{8,4},{9,5},... | collective-permute-start | bytes 491528 | tf_op jit(solution)/shard_map/ppermute | solution.py:131
  79.9 3.0 %collective-permute-done.4 = bf16[80,2048]{1,0:T(8,128)(2,1)S(1)} collective-permute-done((bf16[80,2048]{1,0:T(8,128)(2,1)S(1)}, bf16[80,2048]{1,0:T(8,128)(2,1)S(1)}, u32[]{:S(2)}, u32[]{:S(2)}) %collective-permute-start.4) | collective-permute-done | bytes 327712 | tf_op jit(solution)/shard_map/ppermute | solution.py:152
  83.7 4.3 %collective-permute-start.5 = (bf16[40,2048]{1,0:T(8,128)(2,1)S(1)}, bf16[40,2048]{1,0:T(8,128)(2,1)S(1)}, u32[]{:S(2)}, u32[]{:S(2)}) collective-permute-start(bf16[40,2048]{1,0:T(8,128)(2,1)S(1)} %get-tuple-element.13), channel_id=1, source_target_pairs={{0,4},{1,5},{2,6},{3,7},{4,0},{5,1},{6,2},{7,3},{8,12},{9,13},{10,... | collective-permute-start | bytes 491528 | tf_op jit(solution)/shard_map/ppermute | solution.py:131
  88.0 3.3 %collective-permute-done.5.refs_1_ = bf16[40,2048]{1,0:T(8,128)(2,1)S(1)} collective-permute-done((bf16[40,2048]{1,0:T(8,128)(2,1)S(1)}, bf16[40,2048]{1,0:T(8,128)(2,1)S(1)}, u32[]{:S(2)}, u32[]{:S(2)}) %collective-permute-start.5) | collective-permute-done | bytes 163872 | tf_op jit(solution)/shard_map/ppermute | solution.py:131
  92.0 2.9 %shard_map.62 = bf16[128,2048]{1,0:T(8,128)(2,1)} custom-call(s32[1]{0:T(128)} %bitcast.here_ref, s32[1,128]{1,0:T(1,128)} %bitcast.4, f32[1,128]{1,0:T(1,128)} %bitcast.5, bf16[40,2048]{1,0:T(8,128)(2,1)} %get-tuple-element.14.refs_0_, bf16[40,2048]{1,0:T(8,128)(2,1)} %copy-done.5, bf16[40,2048]{1,0:T(8,128)(2,1)} %copy-done.3, bf16[40,2048]{1,0:T(8,128)(2,1)} %copy-done.4), custom_call_target="tpu_custom_call" | custom-call | tf_op jit(solution)/shard_map/pallas_call | solution.py:157
  (42 shorter events, 5.0 us)
Async XLA Ops:
  2.3 10.0 %collective-permute-start = (bf16[40,2048]{1,0:T(8,128)(2,1)}, bf16[40,2048]{1,0:T(8,128)(2,1)S(1)}, u32[]{:S(2)}, u32[]{:S(2)}) collective-permute-start(bf16[40,2048]{1,0:T(8,128)(2,1)} %get-tuple-element.10), channel_id=1, source_target_pairs={{0,4},{1,5},{2,6},{3,7},{4,0},{5,1},{6,2},{7,3},{8,12},{9,13},{10,... | collective-permute-start | bytes 491528 | tf_op jit(solution)/shard_map/ppermute | solution.py:131
  5.3 15.2 %collective-permute-start.6 = (bf16[40,2048]{1,0:T(8,128)(2,1)}, bf16[40,2048]{1,0:T(8,128)(2,1)S(1)}, u32[]{:S(2)}, u32[]{:S(2)}) collective-permute-start(bf16[40,2048]{1,0:T(8,128)(2,1)} %get-tuple-element.11), channel_id=1, source_target_pairs={{0,8},{1,9},{2,10},{3,11},{4,12},{5,13},{6,14},{7,15},{8,0},{9,1},... | collective-permute-start | bytes 491528 | tf_op jit(solution)/shard_map/ppermute | solution.py:131
  7.9 11.1 %collective-permute-start.12 = (bf16[40,2048]{1,0:T(8,128)(2,1)}, bf16[40,2048]{1,0:T(8,128)(2,1)S(1)}, u32[]{:S(2)}, u32[]{:S(2)}) collective-permute-start(bf16[40,2048]{1,0:T(8,128)(2,1)} %get-tuple-element.12), channel_id=1, source_target_pairs={{0,12},{1,13},{2,14},{3,15},{4,8},{5,9},{6,10},{7,11},{8,4},{9,5},... | collective-permute-start | bytes 491528 | tf_op jit(solution)/shard_map/ppermute | solution.py:131
  13.2 30.6 %collective-permute-start.1 = (bf16[80,2048]{1,0:T(8,128)(2,1)S(1)}, bf16[80,2048]{1,0:T(8,128)(2,1)S(1)}, u32[]{:S(2)}, u32[]{:S(2)}) collective-permute-start(bf16[80,2048]{1,0:T(8,128)(2,1)S(1)} %pad_maximum_fusion), channel_id=1, source_target_pairs={{0,1},{1,0},{2,3},{3,2},{4,5},{5,4},{6,7},{7,6},{8,9},{9,8},{10,11... | collective-permute-start | bytes 983048 | tf_op jit(solution)/shard_map/ppermute | solution.py:146
  19.1 8.7 %collective-permute-start.13 = (bf16[40,2048]{1,0:T(8,128)(2,1)S(1)}, bf16[40,2048]{1,0:T(8,128)(2,1)S(1)}, u32[]{:S(2)}, u32[]{:S(2)}) collective-permute-start(bf16[40,2048]{1,0:T(8,128)(2,1)S(1)} %collective-permute-done.12), channel_id=1, source_target_pairs={{0,1},{1,0},{2,3},{3,2},{4,5},{5,4},{6,7},{7,6},{8,9},{9,8},{10,11... | collective-permute-start | bytes 491528 | tf_op jit(solution)/shard_map/ppermute | solution.py:146
  20.6 5.6 %collective-permute-start.7 = (bf16[40,2048]{1,0:T(8,128)(2,1)S(1)}, bf16[40,2048]{1,0:T(8,128)(2,1)S(1)}, u32[]{:S(2)}, u32[]{:S(2)}) collective-permute-start(bf16[40,2048]{1,0:T(8,128)(2,1)S(1)} %collective-permute-done.6), channel_id=1, source_target_pairs={{0,1},{1,0},{2,3},{3,2},{4,5},{5,4},{6,7},{7,6},{8,9},{9,8},{10,11... | collective-permute-start | bytes 491528 | tf_op jit(solution)/shard_map/ppermute | solution.py:146
  26.2 12.9 %collective-permute-start.8 = (bf16[80,2048]{1,0:T(8,128)(2,1)S(1)}, bf16[80,2048]{1,0:T(8,128)(2,1)S(1)}, u32[]{:S(2)}, u32[]{:S(2)}) collective-permute-start(bf16[80,2048]{1,0:T(8,128)(2,1)S(1)} %constant_dynamic-update-slice_fusion.3.rows_ref), channel_id=1, source_target_pairs={{0,2},{1,3},{2,0},{3,1},{4,6},{5,7},{6,4},{7,5},{8,10},{9,11},{10,... | collective-permute-start | bytes 983048 | tf_op jit(solution)/shard_map/ppermute | solution.py:147
  27.8 20.3 %collective-permute-start.14 = (bf16[80,2048]{1,0:T(8,128)(2,1)S(1)}, bf16[80,2048]{1,0:T(8,128)(2,1)S(1)}, u32[]{:S(2)}, u32[]{:S(2)}) collective-permute-start(bf16[80,2048]{1,0:T(8,128)(2,1)S(1)} %constant_dynamic-update-slice_fusion.5.rows_ref), channel_id=1, source_target_pairs={{0,2},{1,3},{2,0},{3,1},{4,6},{5,7},{6,4},{7,5},{8,10},{9,11},{10,... | collective-permute-start | bytes 983048 | tf_op jit(solution)/shard_map/ppermute | solution.py:147
  28.3 2.2 %copy-start = (bf16[2048,1024]{1,0:T(8,128)(2,1)S(1)}, bf16[2048,1024]{1,0:T(8,128)(2,1)}, u32[]{:S(2)}) copy-start(bf16[2048,1024]{1,0:T(8,128)(2,1)} %weight_in_ref.11) | copy-start | bytes 12582916
  30.5 2.2 %copy-start.2 = (bf16[1024,2048]{1,0:T(8,128)(2,1)S(1)}, bf16[1024,2048]{1,0:T(8,128)(2,1)}, u32[]{:S(2)}) copy-start(bf16[1024,2048]{1,0:T(8,128)(2,1)} %weight_out_ref.11) | copy-start | bytes 12582916
  42.3 10.6 %collective-permute-start.9 = (bf16[80,2048]{1,0:T(8,128)(2,1)S(1)}, bf16[80,2048]{1,0:T(8,128)(2,1)S(1)}, u32[]{:S(2)}, u32[]{:S(2)}) collective-permute-start(bf16[80,2048]{1,0:T(8,128)(2,1)S(1)} %shard_map.59), channel_id=1, source_target_pairs={{0,2},{1,3},{2,0},{3,1},{4,6},{5,7},{6,4},{7,5},{8,10},{9,11},{10,... | collective-permute-start | bytes 983048 | tf_op jit(solution)/shard_map/ppermute | solution.py:150
  43.9 14.3 %collective-permute-start.2 = (bf16[160,2048]{1,0:T(8,128)(2,1)S(1)}, bf16[160,2048]{1,0:T(8,128)(2,1)S(1)}, u32[]{:S(2)}, u32[]{:S(2)}) collective-permute-start(bf16[160,2048]{1,0:T(8,128)(2,1)S(1)} %constant_dynamic-update-slice_fusion.rows_ref), channel_id=1, source_target_pairs={{0,2},{1,3},{2,0},{3,1},{4,6},{5,7},{6,4},{7,5},{8,10},{9,11},{10,... | collective-permute-start | bytes 1966088 | tf_op jit(solution)/shard_map/ppermute | solution.py:147
  48.1 10.1 %copy-start.1 = (bf16[2048,1024]{1,0:T(8,128)(2,1)S(1)}, bf16[2048,1024]{1,0:T(8,128)(2,1)}, u32[]{:S(2)}) copy-start(bf16[2048,1024]{1,0:T(8,128)(2,1)} %weight_in_ref.11) | copy-start | bytes 12582916
  51.3 12.1 %collective-permute-start.15 = (bf16[80,2048]{1,0:T(8,128)(2,1)S(1)}, bf16[80,2048]{1,0:T(8,128)(2,1)S(1)}, u32[]{:S(2)}, u32[]{:S(2)}) collective-permute-start(bf16[80,2048]{1,0:T(8,128)(2,1)S(1)} %shard_map.61), channel_id=1, source_target_pairs={{0,2},{1,3},{2,0},{3,1},{4,6},{5,7},{6,4},{7,5},{8,10},{9,11},{10,... | collective-permute-start | bytes 983048 | tf_op jit(solution)/shard_map/ppermute | solution.py:150
  53.0 12.1 %collective-permute-start.10 = (bf16[40,2048]{1,0:T(8,128)(2,1)S(1)}, bf16[40,2048]{1,0:T(8,128)(2,1)S(1)}, u32[]{:S(2)}, u32[]{:S(2)}) collective-permute-start(bf16[40,2048]{1,0:T(8,128)(2,1)S(1)} %slice.57), channel_id=1, source_target_pairs={{0,1},{1,0},{2,3},{3,2},{4,5},{5,4},{6,7},{7,6},{8,9},{9,8},{10,11... | collective-permute-start | bytes 491528 | tf_op jit(solution)/shard_map/ppermute | solution.py:152
  61.8 13.7 %collective-permute-start.3 = (bf16[160,2048]{1,0:T(8,128)(2,1)S(1)}, bf16[160,2048]{1,0:T(8,128)(2,1)S(1)}, u32[]{:S(2)}, u32[]{:S(2)}) collective-permute-start(bf16[160,2048]{1,0:T(8,128)(2,1)S(1)} %shard_map.57), channel_id=1, source_target_pairs={{0,2},{1,3},{2,0},{3,1},{4,6},{5,7},{6,4},{7,5},{8,10},{9,11},{10,... | collective-permute-start | bytes 1966088 | tf_op jit(solution)/shard_map/ppermute | solution.py:150
  63.5 13.8 %collective-permute-start.16 = (bf16[40,2048]{1,0:T(8,128)(2,1)S(1)}, bf16[40,2048]{1,0:T(8,128)(2,1)S(1)}, u32[]{:S(2)}, u32[]{:S(2)}) collective-permute-start(bf16[40,2048]{1,0:T(8,128)(2,1)S(1)} %slice.56), channel_id=1, source_target_pairs={{0,1},{1,0},{2,3},{3,2},{4,5},{5,4},{6,7},{7,6},{8,9},{9,8},{10,11... | collective-permute-start | bytes 491528 | tf_op jit(solution)/shard_map/ppermute | solution.py:152
  65.1 22.9 %collective-permute-start.11 = (bf16[40,2048]{1,0:T(8,128)(2,1)S(1)}, bf16[40,2048]{1,0:T(8,128)(2,1)S(1)}, u32[]{:S(2)}, u32[]{:S(2)}) collective-permute-start(bf16[40,2048]{1,0:T(8,128)(2,1)S(1)} %fusion.2), channel_id=1, source_target_pairs={{0,8},{1,9},{2,10},{3,11},{4,12},{5,13},{6,14},{7,15},{8,0},{9,1},... | collective-permute-start | bytes 491528 | tf_op jit(solution)/shard_map/ppermute | solution.py:131
  75.8 7.1 %collective-permute-start.4 = (bf16[80,2048]{1,0:T(8,128)(2,1)S(1)}, bf16[80,2048]{1,0:T(8,128)(2,1)S(1)}, u32[]{:S(2)}, u32[]{:S(2)}) collective-permute-start(bf16[80,2048]{1,0:T(8,128)(2,1)S(1)} %slice.55), channel_id=1, source_target_pairs={{0,1},{1,0},{2,3},{3,2},{4,5},{5,4},{6,7},{7,6},{8,9},{9,8},{10,11... | collective-permute-start | bytes 983048 | tf_op jit(solution)/shard_map/ppermute | solution.py:152
  77.4 10.7 %collective-permute-start.17 = (bf16[40,2048]{1,0:T(8,128)(2,1)S(1)}, bf16[40,2048]{1,0:T(8,128)(2,1)S(1)}, u32[]{:S(2)}, u32[]{:S(2)}) collective-permute-start(bf16[40,2048]{1,0:T(8,128)(2,1)S(1)} %fusion.1), channel_id=1, source_target_pairs={{0,12},{1,13},{2,14},{3,15},{4,8},{5,9},{6,10},{7,11},{8,4},{9,5},... | collective-permute-start | bytes 491528 | tf_op jit(solution)/shard_map/ppermute | solution.py:131
  83.7 7.6 %collective-permute-start.5 = (bf16[40,2048]{1,0:T(8,128)(2,1)S(1)}, bf16[40,2048]{1,0:T(8,128)(2,1)S(1)}, u32[]{:S(2)}, u32[]{:S(2)}) collective-permute-start(bf16[40,2048]{1,0:T(8,128)(2,1)S(1)} %get-tuple-element.13), channel_id=1, source_target_pairs={{0,4},{1,5},{2,6},{3,7},{4,0},{5,1},{6,2},{7,3},{8,12},{9,13},{10,... | collective-permute-start | bytes 491528 | tf_op jit(solution)/shard_map/ppermute | solution.py:131
  88.0 3.3 %copy-start.3 = (bf16[40,2048]{1,0:T(8,128)(2,1)}, bf16[40,2048]{1,0:T(8,128)(2,1)S(1)}, u32[]{:S(2)}) copy-start(bf16[40,2048]{1,0:T(8,128)(2,1)S(1)} %collective-permute-done.11.refs_2_) | copy-start | bytes 491524
  88.0 3.3 %copy-start.4 = (bf16[40,2048]{1,0:T(8,128)(2,1)}, bf16[40,2048]{1,0:T(8,128)(2,1)S(1)}, u32[]{:S(2)}) copy-start(bf16[40,2048]{1,0:T(8,128)(2,1)S(1)} %collective-permute-done.17.refs_3_) | copy-start | bytes 491524
  91.3 0.7 copy-start.5
